TPU v7x, 128 devices: a whole 4x4x4 slice. The times are simulated.
128 devices in a mesh: dp: 1, sp: 128 (over z, y, x, core).
Axes of the slice: x: 4, y: 4, z: 4, core: 2. Of those that a mesh axis runs over, the one named last changes fastest.
Arguments:
- signal: bfloat16 [64, 4096, 512], P('dp', 'sp')
- cond_feats: bfloat16 [64, 4096, 256], P('dp', 'sp')
- w_now: bfloat16 [10, 512, 1024], replicated
- w_past: bfloat16 [10, 512, 1024], replicated
- w_cond: bfloat16 [10, 256, 1024], replicated
- b_gate: float32 [10, 1024], replicated
- w_res: bfloat16 [10, 512, 512], replicated
- w_skip: bfloat16 [10, 512, 256], replicated
Outputs:
- output 1: float32 [64, 4096, 512], P('dp', 'sp')
- output 2: float32 [64, 4096, 256], P('dp', 'sp')
All inputs are finite; a program needn't handle non-finite values.
Results may differ from a plain program's by a relative error of at most 0.00665394.
Values are sent between devices in bfloat16 or wider.
A program may use at most 1 GiB of HBM per device.

v0:
```python
import functools

import jax
import jax.numpy as jnp
from jax import lax
from jax.experimental import pallas as pl
from jax.experimental.pallas import tpu as pltpu
from jax.sharding import PartitionSpec as P

LAYERS = 10
NEAR = 5
RING = 8
BLOCKS = 16
CHUNKS = 4
SPAN = 32
ROWS = BLOCKS * SPAN
HALF = ROWS // 2
PAD = 2 * SPAN
CH = 512
COND = 256
SKIP = 256
MESH = pl.DeviceIdType.MESH


def kernel(sig, cond, w_now, w_past, w_cond, bias, w_res, w_skip, h_out, s_out,
           wz, wr, ws, h, skip, cnd, ub, far, shifted, edge_out, edge_in,
           w_sem, own_sem, in_send, in_recv, edge_send, edge_recv, far_send, far_recv, out_send, out_recv, out_own):
    me = lax.axis_index('sp')
    row, lane = me // RING, lax.rem(me, RING)

    def ring(step):
        return {'sp': row * RING + lax.rem(lane + step, RING)}

    def peer(step):
        return lax.rem(row + step, BLOCKS)

    def hop(k):
        return 1 if k <= NEAR else 2 ** (k - NEAR)

    def weight_copies(k):
        return [pltpu.make_async_copy(w_now.at[k], wz.at[k, pl.ds(0, CH)], w_sem.at[k, 0]),
                pltpu.make_async_copy(w_past.at[k], wz.at[k, pl.ds(CH, CH)], w_sem.at[k, 1]),
                pltpu.make_async_copy(w_cond.at[k], wz.at[k, pl.ds(2 * CH, COND)], w_sem.at[k, 2]),
                pltpu.make_async_copy(w_res.at[k], wr.at[k], w_sem.at[k, 3]),
                pltpu.make_async_copy(w_skip.at[k], ws.at[k], w_sem.at[k, 4])]

    def block(b, start=0):
        return pl.ds(pl.multiple_of(start + b * SPAN, SPAN), SPAN)

    def own_inputs(c):
        seq = row * CHUNKS + c
        return [pltpu.make_async_copy(sig.at[seq], ub.at[0, c, block(row, PAD)], own_sem.at[c, 0]),
                pltpu.make_async_copy(cond.at[seq], cnd.at[c, block(row)], own_sem.at[c, 1])]

    def peer_inputs(c, step):
        to = peer(step)
        seq = to * CHUNKS + c
        dev = {'sp': to * RING + lane}
        return [pltpu.make_async_remote_copy(sig.at[seq], ub.at[0, c, block(row, PAD)], in_send.at[c, 0],
                                             in_recv.at[c, 0], device_id=dev, device_id_type=MESH),
                pltpu.make_async_remote_copy(cond.at[seq], cnd.at[c, block(row)], in_send.at[c, 1],
                                             in_recv.at[c, 1], device_id=dev, device_id_type=MESH)]

    def all_inputs(c):
        others = pl.ds(0, ROWS - SPAN)
        return [pltpu.make_async_remote_copy(ub.at[0, c, others], ub.at[0, c, others], in_send.at[c, 0],
                                             in_recv.at[c, 0], device_id=ring(1), device_id_type=MESH),
                pltpu.make_async_remote_copy(cnd.at[c, others], cnd.at[c, others], in_send.at[c, 1],
                                             in_recv.at[c, 1], device_id=ring(1), device_id_type=MESH)]

    def own_outputs(c):
        seq = row * CHUNKS + c
        return [pltpu.make_async_copy(h.at[c, block(row)], h_out.at[seq], out_own.at[c, 0]),
                pltpu.make_async_copy(skip.at[c, block(row)], s_out.at[seq], out_own.at[c, 1])]

    def peer_outputs(c, step):
        to = peer(step)
        seq = row * CHUNKS + c
        dev = {'sp': to * RING + lane}
        return [pltpu.make_async_remote_copy(h.at[c, block(to)], h_out.at[seq], out_send.at[c, 0],
                                             out_recv.at[c, 0], device_id=dev, device_id_type=MESH),
                pltpu.make_async_remote_copy(skip.at[c, block(to)], s_out.at[seq], out_send.at[c, 1],
                                             out_recv.at[c, 1], device_id=dev, device_id_type=MESH)]

    def all_outputs(c):
        others = pl.ds(0, BLOCKS - 1)
        return [pltpu.make_async_remote_copy(h_out.at[others], h_out.at[others], out_send.at[c, 0],
                                             out_recv.at[c, 0], device_id=ring(1), device_id_type=MESH),
                pltpu.make_async_remote_copy(s_out.at[others], s_out.at[others], out_send.at[c, 1],
                                             out_recv.at[c, 1], device_id=ring(1), device_id_type=MESH)]

    def edge_copy(k, c):
        rows = pl.ds(BLOCKS * (2 ** k - 1), BLOCKS * 2 ** k)
        return pltpu.make_async_remote_copy(edge_out.at[c, rows], edge_in.at[c, rows], edge_send.at[k, c],
                                            edge_recv.at[k, c], device_id=ring(1), device_id_type=MESH)

    def far_copy(k, c, half):
        return pltpu.make_async_remote_copy(
            ub.at[k % 2, c, pl.ds(PAD + half * HALF, HALF)], far.at[k - NEAR, c, pl.ds(SPAN + half * HALF, HALF)],
            far_send.at[k - NEAR, c, half], far_recv.at[k - NEAR, c, half], device_id=ring(hop(k)), device_id_type=MESH)

    for c in range(CHUNKS):
        for copy in own_inputs(c):
            copy.start()
    for copy in weight_copies(0):
        copy.start()

    barrier = pltpu.get_barrier_semaphore()
    ring_steps = (1, 2, 4, RING - 2, RING - 1)
    for step in ring_steps:
        pl.semaphore_signal(barrier, inc=1, device_id=ring(step), device_id_type=MESH)
    for step in range(1, BLOCKS):
        pl.semaphore_signal(barrier, inc=1, device_id={'sp': peer(step) * RING + lane}, device_id_type=MESH)
    pl.semaphore_wait(barrier, len(ring_steps) + BLOCKS - 1)

    def start_inputs(i, carry):
        c, step = i // (BLOCKS - 1), lax.rem(i, BLOCKS - 1) + 1
        for copy in peer_inputs(c, step):
            copy.start()
        return carry

    lax.fori_loop(0, CHUNKS * (BLOCKS - 1), start_inputs, 0)
    for k in range(1, LAYERS):
        for copy in weight_copies(k):
            copy.start()

    for c in range(CHUNKS):
        for parity in range(2):
            ub[parity, c, pl.ds(0, PAD)] = jnp.zeros((PAD, CH), jnp.bfloat16)
        for k in range(far.shape[0]):
            far[k, c, pl.ds(0, SPAN)] = jnp.zeros((SPAN, CH), jnp.bfloat16)

    lanes = range(CH // 128)

    def send_edges(k, c):
        d = 2 ** k

        def roll(b, carry):
            for t in lanes:
                shifted[c, t, block(b)] = pltpu.roll(h[c, block(b), pl.ds(128 * t, 128)], d, 0)
            return carry

        lax.fori_loop(0, BLOCKS, roll, 0)
        for j in range(d):
            for t in lanes:
                rows = shifted[c, t, pl.ds(j, BLOCKS, stride=SPAN), :]
                edge_out[c, pl.ds(BLOCKS * (d - 1 + j), BLOCKS), pl.ds(128 * t, 128)] = rows.astype(jnp.bfloat16)
        edge_copy(k, c).start()

    def arrive(c):
        for copy in own_inputs(c):
            copy.wait()
        for copy in all_inputs(c):
            copy.wait_recv()
        h[c] = ub[0, c, pl.ds(PAD, ROWS)].astype(jnp.float32)
        send_edges(0, c)

    def receive_edges(k, c):
        d = 2 ** k
        edge_copy(k, c).wait_recv()

        def patch(start):
            for j in range(d):
                for t in lanes:
                    rows = edge_in[c, pl.ds(BLOCKS * (d - 1 + j), BLOCKS), pl.ds(128 * t, 128)]
                    shifted[c, t, pl.ds(start + j, BLOCKS, stride=SPAN), :] = rows.astype(jnp.float32)

        @pl.when(lane > 0)
        def _():
            patch(0)

        @pl.when(lane == 0)
        def _():
            patch(SPAN)
            for t in lanes:
                shifted[c, t, pl.ds(0, d)] = jnp.zeros((d, 128), jnp.float32)

    def compute(k, c, half):
        rows = pl.ds(half * HALF, HALF)
        own = ub[k % 2, c, pl.ds(PAD + half * HALF, HALF)]
        if k < NEAR:
            past = jnp.concatenate([shifted[c, t, rows].astype(jnp.bfloat16) for t in lanes], axis=1)
        elif k < far.shape[0] + NEAR:
            wrapped = (lane < hop(k)).astype(jnp.int32)
            start = pl.multiple_of(SPAN - SPAN * wrapped + half * HALF, SPAN)
            past = far[k - NEAR, c, pl.ds(start, HALF)]
        else:
            past = ub[k % 2, c, pl.ds(PAD - SPAN * (k - 7) + half * HALF, HALF)]
        x = jnp.concatenate([own, past, cnd[c, rows]], axis=1)
        gated = []
        for col in range(0, CH, 256):
            zf = jnp.dot(x, wz[k, :, col:col + 256], preferred_element_type=jnp.float32)
            zg = jnp.dot(x, wz[k, :, CH + col:CH + col + 256], preferred_element_type=jnp.float32)
            zf = zf + bias[k:k + 1, col:col + 256]
            zg = zg + bias[k:k + 1, CH + col:CH + col + 256]
            gated.append((jnp.tanh(zf) * (0.5 * jnp.tanh(0.5 * zg) + 0.5)).astype(jnp.bfloat16))
        a = jnp.concatenate(gated, axis=1)
        for col in range(0, CH, 256):
            cols = pl.ds(col, 256)
            new = h[c, rows, cols] + jnp.dot(a, wr[k, :, col:col + 256], preferred_element_type=jnp.float32)
            h[c, rows, cols] = new
            if k + 1 < LAYERS:
                ub[(k + 1) % 2, c, pl.ds(PAD + half * HALF, HALF), cols] = new.astype(jnp.bfloat16)
        add = jnp.dot(a, ws[k], preferred_element_type=jnp.float32)
        skip[c, rows] = add if k == 0 else skip[c, rows] + add

    def task(k, c):
        @pl.when(c == 0)
        def _():
            for copy in weight_copies(k):
                copy.wait()

        if k == 0:
            arrive(c)
        if k < NEAR:
            receive_edges(k, c)
        for half in (0, 1):
            if NEAR <= k < NEAR + far.shape[0]:
                far_copy(k, c, half).wait_recv()
            if NEAR <= k - 1 < NEAR + far.shape[0]:
                far_copy(k - 1, c, half).wait_send()
            compute(k, c, half)
            if NEAR <= k + 1 < NEAR + far.shape[0]:
                far_copy(k + 1, c, half).start()
        if k + 1 < NEAR:
            send_edges(k + 1, c)
        if k + 1 == LAYERS:
            for copy in own_outputs(c):
                copy.start()

            def start_outputs(i, carry):
                for copy in peer_outputs(c, i + 1):
                    copy.start()
                return carry

            lax.fori_loop(0, BLOCKS - 1, start_outputs, 0)

    def wave(w, carry):
        for k in reversed(range(LAYERS)):
            c = w - k

            @pl.when((c >= 0) & (c < CHUNKS))
            def _():
                task(k, c)
        return carry

    lax.fori_loop(0, LAYERS + CHUNKS - 1, wave, 0)

    def finish(c, carry):
        for copy in all_inputs(c):
            copy.wait_send()
        for k in range(NEAR):
            edge_copy(k, c).wait_send()
        for copy in own_outputs(c):
            copy.wait()
        for copy in all_outputs(c):
            copy.wait_send()
            copy.wait_recv()
        return carry

    lax.fori_loop(0, CHUNKS, finish, 0)


def solution(mesh):
    def local(signal, cond_feats, w_now, w_past, w_cond, b_gate, w_res, w_skip):
        hbm = pl.BlockSpec(memory_space=pl.ANY)
        dma = pltpu.SemaphoreType.DMA
        return pl.pallas_call(
            kernel,
            out_shape=(jax.ShapeDtypeStruct(signal.shape, jnp.float32),
                       jax.ShapeDtypeStruct(signal.shape[:2] + (SKIP,), jnp.float32)),
            in_specs=[hbm] * 5 + [pl.BlockSpec(memory_space=pltpu.VMEM)] + [hbm] * 2,
            out_specs=(hbm, hbm),
            scratch_shapes=[
                pltpu.VMEM((LAYERS, 2 * CH + COND, 2 * CH), jnp.bfloat16),
                pltpu.VMEM((LAYERS, CH, CH), jnp.bfloat16),
                pltpu.VMEM((LAYERS, CH, SKIP), jnp.bfloat16),
                pltpu.VMEM((CHUNKS, ROWS, CH), jnp.float32),
                pltpu.VMEM((CHUNKS, ROWS, SKIP), jnp.float32),
                pltpu.VMEM((CHUNKS, ROWS, COND), jnp.bfloat16),
                pltpu.VMEM((2, CHUNKS, PAD + ROWS, CH), jnp.bfloat16),
                pltpu.VMEM((3, CHUNKS, SPAN + ROWS, CH), jnp.bfloat16),
                pltpu.VMEM((CHUNKS, CH // 128, SPAN + ROWS, 128), jnp.float32),
                pltpu.VMEM((CHUNKS, BLOCKS * (SPAN - 1), CH), jnp.bfloat16),
                pltpu.VMEM((CHUNKS, BLOCKS * (SPAN - 1), CH), jnp.bfloat16),
                dma((LAYERS, 5)), dma((CHUNKS, 2)), dma((CHUNKS, 2)), dma((CHUNKS, 2)),
                dma((NEAR, CHUNKS)), dma((NEAR, CHUNKS)), dma((3, CHUNKS, 2)), dma((3, CHUNKS, 2)),
                dma((CHUNKS, 2)), dma((CHUNKS, 2)), dma((CHUNKS, 2)),
            ],
            compiler_params=pltpu.CompilerParams(
                collective_id=0, has_side_effects=True, vmem_limit_bytes=67043328),
        )(signal, cond_feats, w_now, w_past, w_cond, b_gate, w_res, w_skip)

    seq = P('dp', 'sp', None)
    return jax.shard_map(local, mesh=mesh, in_specs=(seq, seq, P(), P(), P(), P(), P(), P()),
                         out_specs=(seq, seq), check_vma=False)
```

profile of v0, /device:TPU:0, one launch (start us, length us, event | category | flops | bytes accessed | tf_op | source)
XLA Modules:
  0.0 257.6 jit_solution(6388480636233997663)
XLA Ops:
  0.6 250.5 %shard_map.95 = (f32[64,32,512]{2,1,0:T(8,128)}, f32[64,32,256]{2,1,0:T(8,128)}) custom-call(bf16[64,32,512]{2,1,0:T(8,128)(2,1)} %sig.1, bf16[64,32,256]{2,1,0:T(8,128)(2,1)} %cond.1, bf16[10,512,1024]{2,1,0:T(8,128)(2,1)} %w_now.1, bf16[10,512,1024]{2,1,0:T(8,128)(2,1)} %w_past.1, bf16[10,256,1024]{2,1,0:T(8,128)(2,1)} %w_cond.1, f32[10,1024]{1,0:T(8,128)} %bias.1, ...), custom_call_target="tpu_custom_call" | custom-call | tf_op jit(solution)/shard_map/pallas_call | solution.py:268
  251.1 0.0 copy-start
  251.1 5.2 %copy.12 = f32[64,32,512]{2,1,0:T(8,128)} copy(f32[64,32,512]{2,1,0:T(8,128)} %get-tuple-element.4) | data formatting | bytes 8388608
  256.3 0.0 copy-done
  256.3 1.3 copy.13
Async XLA Ops:
  251.1 5.2 %copy-start = (f32[64,32,256]{2,1,0:T(8,128)S(1)}, f32[64,32,256]{2,1,0:T(8,128)}, u32[]{:S(2)}) copy-start(f32[64,32,256]{2,1,0:T(8,128)} %get-tuple-element.5) | copy-start | bytes 6291460
where the time goes:
time: 258 us
  Pallas kernels  250 us (97%)
  local copies, waits for them, and re-layouts  6.48 us (3%)
    pallas_call x1, Pallas kernels, local(): pl.pallas_call(kernel, out_shape=(jax.ShapeDtypeStruct(signal.shape, jnp....  250 us
    unnamed x4, local copies, waits for them, and re-layouts  6.48 us

commit v1 on v0

--- a/solution.py
+++ b/solution.py
@@ -16,6 +16,12 @@
 ROWS = BLOCKS * SPAN
 HALF = ROWS // 2
 PAD = 2 * SPAN
+RELAYED = 7
+SLOT_ARRIVE = 0
+SLOTS = (6, 13, 18, 25, 31, 36, 41, 53, 54, 55)
+SLOT_FORWARD = 46
+SKEW = 11
+LAG = 3
 CH = 512
 COND = 256
 SKIP = 256
@@ -23,8 +29,8 @@
 
 
 def kernel(sig, cond, w_now, w_past, w_cond, bias, w_res, w_skip, h_out, s_out,
-           wz, wr, ws, h, skip, cnd, ub, far, shifted, edge_out, edge_in,
-           w_sem, own_sem, in_send, in_recv, edge_send, edge_recv, far_send, far_recv, out_send, out_recv, out_own):
+           wz, wr, ws, h, skip, cnd, ub, far, relay, shifted, edge_out, edge_in,
+           w_sem, own_sem, in_send, in_recv, edge_send, edge_recv, far_send, far_recv, relay_send, relay_recv, out_send, out_recv, out_own):
     me = lax.axis_index('sp')
     row, lane = me // RING, lax.rem(me, RING)
 
@@ -73,8 +79,7 @@
         return [pltpu.make_async_copy(h.at[c, block(row)], h_out.at[seq], out_own.at[c, 0]),
                 pltpu.make_async_copy(skip.at[c, block(row)], s_out.at[seq], out_own.at[c, 1])]
 
-    def peer_outputs(c, step):
-        to = peer(step)
+    def peer_outputs(c, to):
         seq = row * CHUNKS + c
         dev = {'sp': to * RING + lane}
         return [pltpu.make_async_remote_copy(h.at[c, block(to)], h_out.at[seq], out_send.at[c, 0],
@@ -95,9 +100,22 @@
                                             edge_recv.at[k, c], device_id=ring(1), device_id_type=MESH)
 
     def far_copy(k, c, half):
+        rows = pl.ds(half * HALF, HALF)
+        src = relay.at[c, rows] if k == RELAYED else ub.at[k % 2, c, pl.ds(PAD + half * HALF, HALF)]
         return pltpu.make_async_remote_copy(
-            ub.at[k % 2, c, pl.ds(PAD + half * HALF, HALF)], far.at[k - NEAR, c, pl.ds(SPAN + half * HALF, HALF)],
-            far_send.at[k - NEAR, c, half], far_recv.at[k - NEAR, c, half], device_id=ring(hop(k)), device_id_type=MESH)
+            src, far.at[k - NEAR, c, pl.ds(SPAN + half * HALF, HALF)], far_send.at[k - NEAR, c, half],
+            far_recv.at[k - NEAR, c, half], device_id=ring(RING - 2 if k == RELAYED else hop(k)), device_id_type=MESH)
+
+    def relay_copy(c, half):
+        return pltpu.make_async_remote_copy(
+            ub.at[RELAYED % 2, c, pl.ds(PAD + half * HALF, HALF)], relay.at[c, pl.ds(half * HALF, HALF)],
+            relay_send.at[c, half], relay_recv.at[c, half], device_id=ring(RING - 2), device_id_type=MESH)
+
+    def send_far(k, c, half):
+        (relay_copy(c, half) if k == RELAYED else far_copy(k, c, half)).start()
+
+    def wait_sent(k, c, half):
+        (relay_copy(c, half) if k == RELAYED else far_copy(k, c, half)).wait_send()
 
     for c in range(CHUNKS):
         for copy in own_inputs(c):
@@ -106,7 +124,7 @@
         copy.start()
 
     barrier = pltpu.get_barrier_semaphore()
-    ring_steps = (1, 2, 4, RING - 2, RING - 1)
+    ring_steps = (1, 2, RING - 2, RING - 1)
     for step in ring_steps:
         pl.semaphore_signal(barrier, inc=1, device_id=ring(step), device_id_type=MESH)
     for step in range(1, BLOCKS):
@@ -175,17 +193,17 @@
             for t in lanes:
                 shifted[c, t, pl.ds(0, d)] = jnp.zeros((d, 128), jnp.float32)
 
-    def compute(k, c, half):
-        rows = pl.ds(half * HALF, HALF)
-        own = ub[k % 2, c, pl.ds(PAD + half * HALF, HALF)]
+    def compute(k, c, first, count):
+        rows = pl.ds(first, count)
+        own = ub[k % 2, c, pl.ds(PAD + first, count)]
         if k < NEAR:
             past = jnp.concatenate([shifted[c, t, rows].astype(jnp.bfloat16) for t in lanes], axis=1)
         elif k < far.shape[0] + NEAR:
             wrapped = (lane < hop(k)).astype(jnp.int32)
-            start = pl.multiple_of(SPAN - SPAN * wrapped + half * HALF, SPAN)
-            past = far[k - NEAR, c, pl.ds(start, HALF)]
+            start = pl.multiple_of(SPAN - SPAN * wrapped + first, SPAN)
+            past = far[k - NEAR, c, pl.ds(start, count)]
         else:
-            past = ub[k % 2, c, pl.ds(PAD - SPAN * (k - 7) + half * HALF, HALF)]
+            past = ub[k % 2, c, pl.ds(PAD - SPAN * (k - RELAYED) + first, count)]
         x = jnp.concatenate([own, past, cnd[c, rows]], axis=1)
         gated = []
         for col in range(0, CH, 256):
@@ -200,57 +218,90 @@
             new = h[c, rows, cols] + jnp.dot(a, wr[k, :, col:col + 256], preferred_element_type=jnp.float32)
             h[c, rows, cols] = new
             if k + 1 < LAYERS:
-                ub[(k + 1) % 2, c, pl.ds(PAD + half * HALF, HALF), cols] = new.astype(jnp.bfloat16)
+                ub[(k + 1) % 2, c, pl.ds(PAD + first, count), cols] = new.astype(jnp.bfloat16)
         add = jnp.dot(a, ws[k], preferred_element_type=jnp.float32)
         skip[c, rows] = add if k == 0 else skip[c, rows] + add
 
-    def task(k, c):
+    def near_layer(k, c):
         @pl.when(c == 0)
         def _():
             for copy in weight_copies(k):
                 copy.wait()
 
-        if k == 0:
-            arrive(c)
-        if k < NEAR:
-            receive_edges(k, c)
-        for half in (0, 1):
-            if NEAR <= k < NEAR + far.shape[0]:
-                far_copy(k, c, half).wait_recv()
-            if NEAR <= k - 1 < NEAR + far.shape[0]:
-                far_copy(k - 1, c, half).wait_send()
-            compute(k, c, half)
-            if NEAR <= k + 1 < NEAR + far.shape[0]:
-                far_copy(k + 1, c, half).start()
+        receive_edges(k, c)
+        compute(k, c, 0, ROWS)
         if k + 1 < NEAR:
             send_edges(k + 1, c)
+        else:
+            for half in range(2):
+                send_far(NEAR, c, half)
+
+    def far_layer(k, half, c):
+        if half == 0:
+            @pl.when(c == 0)
+            def _():
+                for copy in weight_copies(k):
+                    copy.wait()
+
+        if k <= RELAYED:
+            far_copy(k, c, half).wait_recv()
+        if NEAR <= k - 1 <= RELAYED:
+            wait_sent(k - 1, c, half)
+        compute(k, c, half * HALF, HALF)
+        if k < RELAYED:
+            send_far(k + 1, c, half)
         if k + 1 == LAYERS:
-            for copy in own_outputs(c):
-                copy.start()
+            blocks = BLOCKS // 2
+
+            @pl.when(row // blocks == half)
+            def _():
+                for copy in own_outputs(c):
+                    copy.start()
 
             def start_outputs(i, carry):
-                for copy in peer_outputs(c, i + 1):
-                    copy.start()
+                to = half * blocks + lax.rem(row + i, blocks)
+
+                @pl.when(to != row)
+                def _():
+                    for copy in peer_outputs(c, to):
+                        copy.start()
                 return carry
 
-            lax.fori_loop(0, BLOCKS - 1, start_outputs, 0)
+            lax.fori_loop(0, blocks, start_outputs, 0)
+
+    def forward(half, c):
+        relay_copy(c, half).wait_recv()
+        far_copy(RELAYED, c, half).start()
+
+    steps = [(SLOT_ARRIVE, -1, arrive)]
+    for k in range(NEAR):
+        steps.append((SLOTS[k], k, functools.partial(near_layer, k)))
+    for half in range(2):
+        steps.append((SLOT_FORWARD + LAG * half, RELAYED - 0.5 - half / 10, functools.partial(forward, half)))
+        for k in range(NEAR, LAYERS):
+            steps.append((SLOTS[k] + LAG * half, k - half / 10, functools.partial(far_layer, k, half)))
+    steps.sort(key=lambda step: -step[1])
 
     def wave(w, carry):
-        for k in reversed(range(LAYERS)):
-            c = w - k
-
-            @pl.when((c >= 0) & (c < CHUNKS))
-            def _():
-                task(k, c)
+        for first, _, step in steps:
+            since = w - first + CHUNKS * SKEW
+            c = since // SKEW - CHUNKS
+
+            @pl.when((since >= CHUNKS * SKEW) & (lax.rem(since, SKEW) == 0) & (c < CHUNKS))
+            def _(step=step, c=c):
+                step(c)
         return carry
 
-    lax.fori_loop(0, LAYERS + CHUNKS - 1, wave, 0)
+    waves = max(first for first, _, _ in steps) + SKEW * (CHUNKS - 1) + 1
+    lax.fori_loop(0, waves, wave, 0)
 
     def finish(c, carry):
         for copy in all_inputs(c):
             copy.wait_send()
         for k in range(NEAR):
             edge_copy(k, c).wait_send()
+        for half in range(2):
+            far_copy(RELAYED, c, half).wait_send()
         for copy in own_outputs(c):
             copy.wait()
         for copy in all_outputs(c):
@@ -280,11 +331,13 @@
                 pltpu.VMEM((CHUNKS, ROWS, COND), jnp.bfloat16),
                 pltpu.VMEM((2, CHUNKS, PAD + ROWS, CH), jnp.bfloat16),
                 pltpu.VMEM((3, CHUNKS, SPAN + ROWS, CH), jnp.bfloat16),
+                pltpu.VMEM((CHUNKS, ROWS, CH), jnp.bfloat16),
                 pltpu.VMEM((CHUNKS, CH // 128, SPAN + ROWS, 128), jnp.float32),
                 pltpu.VMEM((CHUNKS, BLOCKS * (SPAN - 1), CH), jnp.bfloat16),
                 pltpu.VMEM((CHUNKS, BLOCKS * (SPAN - 1), CH), jnp.bfloat16),
                 dma((LAYERS, 5)), dma((CHUNKS, 2)), dma((CHUNKS, 2)), dma((CHUNKS, 2)),
                 dma((NEAR, CHUNKS)), dma((NEAR, CHUNKS)), dma((3, CHUNKS, 2)), dma((3, CHUNKS, 2)),
+                dma((CHUNKS, 2)), dma((CHUNKS, 2)),
                 dma((CHUNKS, 2)), dma((CHUNKS, 2)), dma((CHUNKS, 2)),
             ],
             compiler_params=pltpu.CompilerParams(

time: 258 us -> 197 us (0.76)
  the two profiles are of different devices: /device:TPU:0 before, /device:TPU:100 now
where the time goes in v1:
time: 197 us
  Pallas kernels  190 us (96%)
  local copies, waits for them, and re-layouts  6.48 us (3%)
    pallas_call x1, Pallas kernels, local(): pl.pallas_call(kernel, out_shape=(jax.ShapeDtypeStruct(signal.shape, jnp....  190 us
    unnamed x4, local copies, waits for them, and re-layouts  6.48 us

profile of v1, /device:TPU:100, one launch (start us, length us, event | category | flops | bytes accessed | tf_op | source)
XLA Modules:
  0.0 196.9 jit_solution(13026064086343144080)
XLA Ops:
  0.6 189.7 %shard_map.95 = (f32[64,32,512]{2,1,0:T(8,128)}, f32[64,32,256]{2,1,0:T(8,128)}) custom-call(bf16[64,32,512]{2,1,0:T(8,128)(2,1)} %sig.1, bf16[64,32,256]{2,1,0:T(8,128)(2,1)} %cond.1, bf16[10,512,1024]{2,1,0:T(8,128)(2,1)} %w_now.1, bf16[10,512,1024]{2,1,0:T(8,128)(2,1)} %w_past.1, bf16[10,256,1024]{2,1,0:T(8,128)(2,1)} %w_cond.1, f32[10,1024]{1,0:T(8,128)} %bias.1, ...), custom_call_target="tpu_custom_call" | custom-call | tf_op jit(solution)/shard_map/pallas_call | solution.py:319
  190.4 0.0 copy-start
  190.4 5.2 %copy.12 = f32[64,32,512]{2,1,0:T(8,128)} copy(f32[64,32,512]{2,1,0:T(8,128)} %get-tuple-element.4) | data formatting | bytes 8388608
  195.5 0.0 copy-done
  195.6 1.3 copy.13
Async XLA Ops:
  190.4 5.2 %copy-start = (f32[64,32,256]{2,1,0:T(8,128)S(1)}, f32[64,32,256]{2,1,0:T(8,128)}, u32[]{:S(2)}) copy-start(f32[64,32,256]{2,1,0:T(8,128)} %get-tuple-element.5) | copy-start | bytes 6291460

commit v2 on v1

--- a/solution.py
+++ b/solution.py
@@ -17,11 +17,13 @@
 HALF = ROWS // 2
 PAD = 2 * SPAN
 RELAYED = 7
-SLOT_ARRIVE = 0
-SLOTS = (6, 13, 18, 25, 31, 36, 41, 53, 54, 55)
-SLOT_FORWARD = 46
-SKEW = 11
-LAG = 3
+STRAIGHT = 3
+WORD_BASE = 128
+WORD_STEPS = 4
+ORDER = (
+    16794112, 4343301, 42156816, 101056913, 15141514, 52954932, 23878674, 84250276,
+    135091772, 142855457, 78093490, 113985961, 71688381, 80645573, 130864938, 116494274,
+    132896167, 268428227)
 CH = 512
 COND = 256
 SKIP = 256
@@ -99,23 +101,41 @@
         return pltpu.make_async_remote_copy(edge_out.at[c, rows], edge_in.at[c, rows], edge_send.at[k, c],
                                             edge_recv.at[k, c], device_id=ring(1), device_id_type=MESH)
 
-    def far_copy(k, c, half):
-        rows = pl.ds(half * HALF, HALF)
-        src = relay.at[c, rows] if k == RELAYED else ub.at[k % 2, c, pl.ds(PAD + half * HALF, HALF)]
+    def far_copy(k, c, half, src=None, to=None):
+        if src is None:
+            src = ub.at[k % 2, c, pl.ds(PAD + half * HALF, HALF)]
         return pltpu.make_async_remote_copy(
             src, far.at[k - NEAR, c, pl.ds(SPAN + half * HALF, HALF)], far_send.at[k - NEAR, c, half],
-            far_recv.at[k - NEAR, c, half], device_id=ring(RING - 2 if k == RELAYED else hop(k)), device_id_type=MESH)
+            far_recv.at[k - NEAR, c, half], device_id=ring(hop(k) if to is None else to), device_id_type=MESH)
+
+    def forward_copy(c, half):
+        return far_copy(RELAYED, c, half, relay.at[c, pl.ds(half * HALF, HALF)], RING - 2)
 
     def relay_copy(c, half):
         return pltpu.make_async_remote_copy(
             ub.at[RELAYED % 2, c, pl.ds(PAD + half * HALF, HALF)], relay.at[c, pl.ds(half * HALF, HALF)],
             relay_send.at[c, half], relay_recv.at[c, half], device_id=ring(RING - 2), device_id_type=MESH)
 
+    def on_route(c, relayed, straight):
+        @pl.when(c < STRAIGHT)
+        def _():
+            relayed()
+
+        @pl.when(c >= STRAIGHT)
+        def _():
+            straight()
+
     def send_far(k, c, half):
-        (relay_copy(c, half) if k == RELAYED else far_copy(k, c, half)).start()
+        if k == RELAYED:
+            on_route(c, relay_copy(c, half).start, far_copy(k, c, half).start)
+        else:
+            far_copy(k, c, half).start()
 
     def wait_sent(k, c, half):
-        (relay_copy(c, half) if k == RELAYED else far_copy(k, c, half)).wait_send()
+        if k == RELAYED:
+            on_route(c, relay_copy(c, half).wait_send, far_copy(k, c, half).wait_send)
+        else:
+            far_copy(k, c, half).wait_send()
 
     for c in range(CHUNKS):
         for copy in own_inputs(c):
@@ -124,7 +144,7 @@
         copy.start()
 
     barrier = pltpu.get_barrier_semaphore()
-    ring_steps = (1, 2, RING - 2, RING - 1)
+    ring_steps = (1, 2, 4, RING - 2, RING - 1)
     for step in ring_steps:
         pl.semaphore_signal(barrier, inc=1, device_id=ring(step), device_id_type=MESH)
     for step in range(1, BLOCKS):
@@ -271,37 +291,43 @@
 
     def forward(half, c):
         relay_copy(c, half).wait_recv()
-        far_copy(RELAYED, c, half).start()
-
-    steps = [(SLOT_ARRIVE, -1, arrive)]
-    for k in range(NEAR):
-        steps.append((SLOTS[k], k, functools.partial(near_layer, k)))
+        forward_copy(c, half).start()
+
+    steps = [arrive] + [functools.partial(near_layer, k) for k in range(NEAR)]
     for half in range(2):
-        steps.append((SLOT_FORWARD + LAG * half, RELAYED - 0.5 - half / 10, functools.partial(forward, half)))
-        for k in range(NEAR, LAYERS):
-            steps.append((SLOTS[k] + LAG * half, k - half / 10, functools.partial(far_layer, k, half)))
-    steps.sort(key=lambda step: -step[1])
-
-    def wave(w, carry):
-        for first, _, step in steps:
-            since = w - first + CHUNKS * SKEW
-            c = since // SKEW - CHUNKS
-
-            @pl.when((since >= CHUNKS * SKEW) & (lax.rem(since, SKEW) == 0) & (c < CHUNKS))
-            def _(step=step, c=c):
-                step(c)
+        steps += [functools.partial(far_layer, k, half) for k in range(NEAR, RELAYED)]
+        steps += [functools.partial(forward, half)]
+        steps += [functools.partial(far_layer, k, half) for k in range(RELAYED, LAYERS)]
+
+    def run_word(i, carry):
+        word = sum(jnp.where(i == j, packed, 0) for j, packed in enumerate(ORDER))
+
+        def run_step(_, word):
+            step, c = lax.div(lax.rem(word, WORD_BASE), CHUNKS), lax.rem(word, CHUNKS)
+            for start in range(0, len(steps), 5):
+                @pl.when((step >= start) & (step < start + 5))
+                def _(start=start):
+                    for index in range(start, min(start + 5, len(steps))):
+                        @pl.when(step == index)
+                        def _(index=index):
+                            steps[index](c)
+            return lax.div(word, WORD_BASE)
+
+        lax.fori_loop(0, WORD_STEPS, run_step, word)
         return carry
 
-    waves = max(first for first, _, _ in steps) + SKEW * (CHUNKS - 1) + 1
-    lax.fori_loop(0, waves, wave, 0)
+    lax.fori_loop(0, len(ORDER), run_word, 0)
 
     def finish(c, carry):
         for copy in all_inputs(c):
             copy.wait_send()
         for k in range(NEAR):
             edge_copy(k, c).wait_send()
-        for half in range(2):
-            far_copy(RELAYED, c, half).wait_send()
+        @pl.when(c < STRAIGHT)
+        def _():
+            for half in range(2):
+                forward_copy(c, half).wait_send()
+
         for copy in own_outputs(c):
             copy.wait()
         for copy in all_outputs(c):

time: 197 us -> 192 us (0.975)
  Pallas kernels: 190 us -> 184 us
    pallas_call x1, Pallas kernels: 190 us -> 184 us  [local(): pl.pallas_call(kernel, out_shape=(jax.ShapeDtypeStruct(signal.shape, jnp....]
where the time goes in v2:
time: 192 us; the launch traced here: 191 us
  Pallas kernels  184 us (96%)
  local copies, waits for them, and re-layouts  6.48 us (3%)
    pallas_call x1, Pallas kernels, local(): pl.pallas_call(kernel, out_shape=(jax.ShapeDtypeStruct(signal.shape, jnp....  184 us
    unnamed x4, local copies, waits for them, and re-layouts  6.48 us

profile of v2, /device:TPU:100, one launch (start us, length us, event | category | flops | bytes accessed | tf_op | source)
XLA Modules:
  0.0 191.4 jit_solution(17765775468536040799)
XLA Ops:
  0.6 184.3 %shard_map.95 = (f32[64,32,512]{2,1,0:T(8,128)}, f32[64,32,256]{2,1,0:T(8,128)}) custom-call(bf16[64,32,512]{2,1,0:T(8,128)(2,1)} %sig.1, bf16[64,32,256]{2,1,0:T(8,128)(2,1)} %cond.1, bf16[10,512,1024]{2,1,0:T(8,128)(2,1)} %w_now.1, bf16[10,512,1024]{2,1,0:T(8,128)(2,1)} %w_past.1, bf16[10,256,1024]{2,1,0:T(8,128)(2,1)} %w_cond.1, f32[10,1024]{1,0:T(8,128)} %bias.1, ...), custom_call_target="tpu_custom_call" | custom-call | tf_op jit(solution)/shard_map/pallas_call | solution.py:345
  185.0 0.0 copy-start
  185.0 5.2 %copy.12 = f32[64,32,512]{2,1,0:T(8,128)} copy(f32[64,32,512]{2,1,0:T(8,128)} %get-tuple-element.4) | data formatting | bytes 8388608
  190.1 0.0 copy-done
  190.1 1.3 copy.13
Async XLA Ops:
  185.0 5.2 %copy-start = (f32[64,32,256]{2,1,0:T(8,128)S(1)}, f32[64,32,256]{2,1,0:T(8,128)}, u32[]{:S(2)}) copy-start(f32[64,32,256]{2,1,0:T(8,128)} %get-tuple-element.5) | copy-start | bytes 6291460
